TPU v7x, 32 devices: a whole 2x2x4 slice. The times are simulated.
32 devices in a mesh: slab: 8 (over z, x), sub: 4 (over y, core).
Axes of the slice: x: 2, y: 2, z: 4, core: 2. Of those that a mesh axis runs over, the one named last changes fastest.
Arguments:
- values: float32 [768, 2, 128, 256], P(('slab', 'sub')), may hold values from -0.25 to 0.25
- block_ids: int32 [768, 2], P(('slab', 'sub')), may hold values from 0 to 383, as said below
- tile_counts: int32 [8, 4], P('slab', 'sub'), may hold values from 8 to 24, as said below
- right_side: float32 [768, 128], P(('slab', 'sub')), may hold values from -18 to 18
Outputs:
- solution: float32 [384, 256], P(('slab', 'sub'))
- residual: float32 [768, 128], P(('slab', 'sub'))
Inputs may be any that keep to these rules, and one draw needn't show every extreme that they name: `block_ids`: every block id names a node block held by a device of the row tile's own slab or of a slab one index of slab away; the first coupled block of each tile lies in its own slab. Block b is held by device b div 12. `tile_counts`: some device has all 24 slots live in every draw.
All inputs are finite; a program needn't handle non-finite values.
Results may differ from a plain program's by a relative error of at most 0.0003.
Values sent between devices are 32-bit elements; how exact they have to be, the bound alone decides.
A program may use at most 64 MiB of HBM per device.

v0:
```python
import functools

import jax
import jax.numpy as jnp
from jax import lax
from jax.experimental import pallas as pl
from jax.experimental.pallas import tpu as pltpu
from jax.sharding import PartitionSpec as P

ITERS = 4
NB_DEV = 12
LANES = 128
MESH = pl.DeviceIdType.MESH


def round_up(size, unit):
    return -(-size // unit) * unit


def kernel(
    n_slab,
    n_sub,
    values_hbm,
    ids_hbm,
    counts_hbm,
    right_hbm,
    solution_ref,
    residual_ref,
    values,
    wid,
    turned,
    selector,
    terms,
    squares,
    image_cols,
    image_rows,
    first_out,
    first_in,
    part_out,
    part_in,
    field_out,
    field_in,
    field_win,
    scal1,
    scal2,
    ids_smem,
    counts_smem,
    right_ref,
    small_sem,
    load_sem,
    first_send,
    first_recv,
    part_send,
    part_recv,
    field_send,
    field_recv,
    scal1_send,
    scal1_recv,
    scal2_send,
    scal2_recv,
):
    tiles, coupled, rows, block = values.shape
    halves = block // LANES
    held = NB_DEV * halves
    n = n_slab * n_sub
    window = 3 * n_sub * held
    f32 = jnp.float32
    slab = lax.axis_index("slab")
    sub = lax.axis_index("sub")
    me = slab * n_sub + sub

    def keeper(s):
        return s + 1 - 2 * lax.rem(s, 2) if n_slab % 2 == 0 else s

    kept = keeper(slab)

    small = [
        pltpu.make_async_copy(src, dst, small_sem.at[i])
        for i, (src, dst) in enumerate(
            ((ids_hbm, ids_smem), (counts_hbm, counts_smem), (right_hbm, right_ref))
        )
    ]
    for copy in small:
        copy.start()
    for t in range(tiles):
        pltpu.make_async_copy(values_hbm.at[t], values.at[t], load_sem.at[t]).start()

    def other(j):
        target = lax.rem(me + j, n)
        return (lax.div(target, n_sub), lax.rem(target, n_sub))

    barrier = pltpu.get_barrier_semaphore()

    @pl.loop(1, n)
    def _(j):
        pl.semaphore_signal(barrier, inc=1, device_id=other(j), device_id_type=MESH)

    for copy in small:
        copy.wait()

    turned[...] = jnp.zeros_like(turned)
    terms[...] = jnp.zeros_like(terms)
    squares[...] = jnp.zeros_like(squares)
    lane_ids = lax.broadcasted_iota(jnp.int32, (1, turned.shape[1]), 1)

    @pl.loop(0, tiles)
    def _(t):
        for k in range(coupled):
            b = ids_smem[t, k]
            owner = lax.div(b, NB_DEV)
            rel = jnp.clip(lax.div(owner, n_sub) - slab + 1, 0, 2)
            row = (rel * n_sub + lax.rem(owner, n_sub)) * held + lax.rem(b, NB_DEV)
            wid[t, k] = row
            for h in range(halves):
                hot = (lane_ids == row + h * NB_DEV).astype(f32)
                turned[pl.ds((k * halves + h) * tiles + t, 1), :] = hot

    selector[...] = turned[...].T.astype(jnp.bfloat16)

    def blank_part(low):
        first_in[low : low + n_sub] = jnp.zeros((n_sub,) + first_in.shape[1:], f32)
        for it in range(part_in.shape[0]):
            part_in[it, low : low + n_sub] = jnp.zeros((n_sub,) + part_in.shape[2:], f32)

    def blank_field(rel):
        for it in range(field_in.shape[0]):
            field_in[it, rel] = jnp.zeros(field_in.shape[2:], f32)

    pl.when(kept == 0)(lambda: blank_part(2 * n_sub))
    pl.when(kept == n_slab - 1)(lambda: blank_part(0))
    pl.when(slab == 0)(lambda: blank_field(0))
    pl.when(slab == n_slab - 1)(lambda: blank_field(2))

    def live(t):
        return jnp.where(t < counts_smem[0, 0], 1.0, 0.0).astype(f32)

    eye = (
        lax.broadcasted_iota(jnp.int32, (rows, LANES), 0)
        == lax.broadcasted_iota(jnp.int32, (rows, LANES), 1)
    ).astype(f32)

    def half(h):
        return slice(h * LANES, (h + 1) * LANES)

    def term_row(k, h, t):
        return pl.ds((k * halves + h) * tiles + t, 1)

    def scatter(term_refs):
        cut = []
        for ref in term_refs:
            rest = ref[...]
            for _ in range(3):
                piece = rest.astype(jnp.bfloat16)
                cut.append(piece)
                rest = rest - piece.astype(f32)
        spread = jnp.dot(
            selector[...], jnp.concatenate(cut, axis=1), preferred_element_type=f32
        )
        outs = []
        for i in range(len(term_refs)):
            a, b, c = (spread[:window, half(3 * i + j)] for j in range(3))
            outs.append((a + (b + c)).reshape(3, n_sub, held, LANES))
        return outs

    def inside(s):
        return jnp.logical_and(s >= 0, s < n_slab)

    def each(act, scatters):
        for ds in (1, -1, 0):
            for step in (*range(1, n_sub), 0):
                if scatters:
                    exists, far = inside(slab + ds), keeper(slab + ds)
                else:
                    exists, far = inside(kept - ds), kept - ds
                if step == 0:
                    exists = jnp.logical_and(exists, far != slab)
                pl.when(exists)(functools.partial(act, ds, step))

    def part_copy(out_ref, in_ref, send, recv, ds, step):
        target = lax.rem(sub + step, n_sub)
        slot = (ds + 1) * n_sub + step
        return pltpu.make_async_remote_copy(
            src_ref=out_ref.at[ds + 1, target],
            dst_ref=in_ref.at[slot],
            send_sem=send.at[slot],
            recv_sem=recv.at[slot],
            device_id=(keeper(slab + ds), target),
            device_id_type=MESH,
        )

    def field_copy(it, ds, step):
        target = lax.rem(sub + step, n_sub)
        slot = (ds + 1) * n_sub + step
        return pltpu.make_async_remote_copy(
            src_ref=field_out.at[it],
            dst_ref=field_in.at[it, ds + 1, sub],
            send_sem=field_send.at[it, slot],
            recv_sem=field_recv.at[it, slot],
            device_id=(kept - ds, target),
            device_id_type=MESH,
        )

    def start_all(copy, scatters):
        each(lambda ds, step: copy(ds, step).start(), scatters)

    def wait_recv_all(copy, scatters):
        each(lambda ds, step: copy(ds, step).wait_recv(), not scatters)

    def wait_send_all(copy, scatters):
        each(lambda ds, step: copy(ds, step).wait_send(), scatters)

    own_rel = kept - slab + 1
    own_slot = own_rel * n_sub

    def scal_copy(ref, send, recv, it, j):
        return pltpu.make_async_remote_copy(
            src_ref=ref.at[it, me],
            dst_ref=ref.at[it, me],
            send_sem=send.at[it],
            recv_sem=recv.at[it],
            device_id=other(j),
            device_id_type=MESH,
        )

    def scal_start(ref, send, recv, it):
        @pl.loop(1, n)
        def _(j):
            scal_copy(ref, send, recv, it, j).start()

    def scal_all(ref, send, recv, it):
        rest = ref.at[it, pl.ds(0, n - 1)]
        return pltpu.make_async_remote_copy(
            src_ref=rest,
            dst_ref=rest,
            send_sem=send.at[it],
            recv_sem=recv.at[it],
            device_id=other(1),
            device_id_type=MESH,
        )

    def total(x):
        return jnp.sum(jnp.sum(x, axis=0, keepdims=True), axis=1, keepdims=True)

    @pl.loop(0, tiles)
    def _(t):
        pltpu.make_async_copy(values_hbm.at[t], values.at[t], load_sem.at[t]).wait()
        alive = live(t)
        cols = jnp.sum(eye * (right_ref[pl.ds(t, 1), :] * alive), axis=1, keepdims=True)
        cols = jnp.broadcast_to(cols, (rows, LANES))
        for k in range(coupled):
            for h in range(halves):
                a = values[t, k, :, half(h)]
                terms[term_row(k, h, t), :] = jnp.sum(a * cols, axis=0, keepdims=True)
                squares[term_row(k, h, t), :] = (
                    jnp.sum(a * a, axis=0, keepdims=True) * alive
                )
        residual_ref[pl.ds(t, 1), :] = right_ref[pl.ds(t, 1), :] * alive

    pieces = scatter((terms, squares))
    for i in range(2):
        first_out[:, :, i] = pieces[i]
    pl.semaphore_wait(barrier, n - 1)
    first_copy = functools.partial(part_copy, first_out, first_in, first_send, first_recv)
    start_all(first_copy, True)
    first_in[own_slot] = first_out[own_rel, sub]
    wait_recv_all(first_copy, True)
    sums = jnp.sum(first_in[...], axis=0)
    normal_res = sums[0]
    jacobi = 1.0 / (1.0 + sums[1])
    scaled = jacobi * normal_res
    field_out[0] = scaled
    rho_part = total(normal_res * scaled)
    scal2[0, me] = jnp.broadcast_to(rho_part, (2, LANES))
    start_all(functools.partial(field_copy, 0), False)
    scal_start(scal2, scal2_send, scal2_recv, 0)
    field_in[0, own_rel, sub] = scaled
    wait_recv_all(functools.partial(field_copy, 0), False)
    answer = jnp.zeros((held, LANES), f32)
    for it in range(ITERS):
        last = it == ITERS - 1
        field_win[...] = field_in[it].reshape(window, LANES)

        def tile_pass(t, carry):
            alive = live(t)
            m = None
            for k in range(coupled):
                for h in range(halves):
                    picked = field_win[pl.ds(wid[t, k] + h * NB_DEV, 1), :] * alive
                    product = values[t, k, :, half(h)] * picked
                    m = product if m is None else m + product
            image = jnp.broadcast_to(jnp.sum(m, axis=1, keepdims=True), (rows, LANES))
            image_cols[t] = image
            if not last:
                for k in range(coupled):
                    for h in range(halves):
                        terms[term_row(k, h, t), :] = jnp.sum(
                            values[t, k, :, half(h)] * image, axis=0, keepdims=True
                        )
            return carry

        lax.fori_loop(0, tiles, tile_pass, 0, unroll=8)
        if not last:
            part_out[it] = scatter((terms,))[0]
            out_copy = functools.partial(
                part_copy, part_out.at[it], part_in.at[it], part_send.at[it], part_recv.at[it]
            )
            part_in[it, own_slot] = part_out[it, own_rel, sub]
            start_all(out_copy, True)

        @pl.loop(0, tiles, unroll=4)
        def _(t):
            image_rows[pl.ds(t, 1), :] = jnp.sum(image_cols[t] * eye, axis=0, keepdims=True)

        field_own = field_in[it, 1, sub]
        if it == 0:
            scal_all(scal2, scal2_send, scal2_recv, 0).wait_recv()
            rho_now = jnp.sum(scal2[0], axis=0)[0:1]
            scaled_own = field_own
            direction = field_own
            scaled_image = image_rows[...]
            image = scaled_image
        else:
            scal_all(scal1, scal1_send, scal1_recv, it - 1).wait_recv()
            step_size = rho_now / jnp.sum(scal1[it - 1], axis=0)
            answer = answer + step_size * direction
            residual_ref[...] = residual_ref[...] - step_size * image
            scaled = scaled - step_size * back_scaled
            scal_all(scal2, scal2_send, scal2_recv, it).wait_recv()
            both = jnp.sum(scal2[it], axis=0)
            rho_next = rho_now - 2.0 * step_size * both[0:1] + step_size * step_size * both[1:2]
            beta = rho_next / rho_now
            rho_now = rho_next
            scaled_own = scaled_own - step_size * field_own
            direction = scaled_own + beta * direction
            scaled_image = scaled_image - step_size * image_rows[...]
            image = scaled_image + beta * image
        scal1[it, me] = jnp.broadcast_to(total(image * image), (1, LANES))
        scal_start(scal1, scal1_send, scal1_recv, it)

        if not last:
            wait_recv_all(out_copy, True)
            spread = jnp.sum(part_in[it], axis=0)
            if it == 0:
                scaled_back = spread
                back = spread
            else:
                scaled_back = scaled_back - step_size * spread
                back = scaled_back + beta * back
            back_scaled = jacobi * back
            field_out[it + 1] = back_scaled
            start_all(functools.partial(field_copy, it + 1), False)
            scal2[it + 1, me, 0:1] = jnp.broadcast_to(total(scaled * back), (1, LANES))
            scal2[it + 1, me, 1:2] = jnp.broadcast_to(total(back * back_scaled), (1, LANES))
            scal_start(scal2, scal2_send, scal2_recv, it + 1)
            field_in[it + 1, own_rel, sub] = back_scaled
            wait_recv_all(functools.partial(field_copy, it + 1), False)

    scal_all(scal1, scal1_send, scal1_recv, ITERS - 1).wait_recv()
    step_size = rho_now / jnp.sum(scal1[ITERS - 1], axis=0)
    answer = answer + step_size * direction
    residual_ref[...] = residual_ref[...] - step_size * image
    for h in range(halves):
        solution_ref[:, half(h)] = answer[h * NB_DEV : (h + 1) * NB_DEV]

    wait_send_all(first_copy, True)
    for it in range(ITERS):
        wait_send_all(functools.partial(field_copy, it), False)
        scal_all(scal1, scal1_send, scal1_recv, it).wait_send()
        scal_all(scal2, scal2_send, scal2_recv, it).wait_send()
        if it < ITERS - 1:
            wait_send_all(
                functools.partial(
                    part_copy, part_out.at[it], part_in.at[it], part_send.at[it], part_recv.at[it]
                ),
                True,
            )


def per_device(n_slab, n_sub, values, block_ids, tile_counts, right_side):
    tiles, coupled, rows, block = values.shape
    halves = block // LANES
    held = NB_DEV * halves
    n = n_slab * n_sub
    slots = 3 * n_sub
    window = slots * held
    n_terms = round_up(tiles * coupled * halves, LANES)
    n_window = round_up(window, LANES)
    f32 = jnp.float32
    vmem = pltpu.VMEM
    dma = pltpu.SemaphoreType.DMA
    whole = pl.BlockSpec(memory_space=pltpu.VMEM)
    return pl.pallas_call(
        functools.partial(kernel, n_slab, n_sub),
        out_shape=(
            jax.ShapeDtypeStruct((NB_DEV, block), f32),
            jax.ShapeDtypeStruct((tiles, rows), f32),
        ),
        in_specs=[pl.BlockSpec(memory_space=pl.ANY)] * 4,
        out_specs=(whole, whole),
        scratch_shapes=[
            vmem(values.shape, f32),
            pltpu.SMEM((tiles, coupled), jnp.int32),
            vmem((n_terms, n_window), f32),
            vmem((n_window, n_terms), jnp.bfloat16),
            vmem((n_terms, LANES), f32),
            vmem((n_terms, LANES), f32),
            vmem((tiles, rows, LANES), f32),
            vmem((tiles, LANES), f32),
            vmem((3, n_sub, 2, held, LANES), f32),
            vmem((slots, 2, held, LANES), f32),
            vmem((ITERS - 1, 3, n_sub, held, LANES), f32),
            vmem((ITERS - 1, slots, held, LANES), f32),
            vmem((ITERS, held, LANES), f32),
            vmem((ITERS, 3, n_sub, held, LANES), f32),
            vmem((window, LANES), f32),
            vmem((ITERS, n, 1, LANES), f32),
            vmem((ITERS, n, 2, LANES), f32),
            pltpu.SMEM((tiles, coupled), jnp.int32),
            pltpu.SMEM((1, 1), jnp.int32),
            vmem((tiles, rows), f32),
            dma((3,)),
            dma((tiles,)),
            dma((slots,)),
            dma((slots,)),
            dma((ITERS - 1, slots)),
            dma((ITERS - 1, slots)),
            dma((ITERS, slots)),
            dma((ITERS, slots)),
            dma((ITERS,)),
            dma((ITERS,)),
            dma((ITERS,)),
            dma((ITERS,)),
        ],
        compiler_params=pltpu.CompilerParams(
            collective_id=0, has_side_effects=True, vmem_limit_bytes=48 * 1024 * 1024
        ),
    )(values, block_ids, tile_counts, right_side)


def solution(mesh):
    in_specs = (
        P(("slab", "sub"), None, None, None),
        P(("slab", "sub"), None),
        P("slab", "sub"),
        P(("slab", "sub"), None),
    )
    out_specs = (P(("slab", "sub"), None), P(("slab", "sub"), None))
    return jax.shard_map(
        functools.partial(per_device, mesh.shape["slab"], mesh.shape["sub"]),
        mesh=mesh,
        in_specs=in_specs,
        out_specs=out_specs,
        check_vma=False,
    )
```

profile of v0, /device:TPU:0, one launch (start us, length us, event | category | flops | bytes accessed | tf_op | source)
XLA Modules:
  0.0 54.6 jit_solution(15587008768296394147)
XLA Ops:
  1.3 0.8 %copy.6.ids_hbm = s32[24,2]{1,0:T(8,128)S(1)} copy(s32[24,2]{0,1:T(2,128)} %param.5) | data formatting | bytes 384 | tf_op args[1]
  2.0 0.0 copy-start
  2.0 0.7 %copy-done = f32[24,128]{1,0:T(8,128)S(1)} copy-done((f32[24,128]{1,0:T(8,128)S(1)}, f32[24,128]{1,0:T(8,128)}, u32[]{:S(2)}) %copy-start) | copy-done | bytes 12312
  2.7 50.7 %shard_map.59 = (f32[12,256]{1,0:T(8,128)S(1)}, f32[24,128]{1,0:T(8,128)S(1)}) custom-call(f32[24,2,128,256]{3,2,1,0:T(8,128)} %values_hbm.1, s32[24,2]{1,0:T(8,128)S(1)} %copy.6.ids_hbm, s32[1,1]{1,0:T(1,128)S(6)} %copy.9.counts_hbm, f32[24,128]{1,0:T(8,128)S(1)} %copy-done), custom_call_target="tpu_custom_call" | custom-call | tf_op jit(solution)/shard_map/pallas_call | solution.py:392
  53.4 0.6 %copy.10 = f32[12,256]{1,0:T(8,128)} copy(f32[12,256]{1,0:T(8,128)S(1)} %get-tuple-element.4) | data formatting | bytes 24576
  54.0 0.6 %copy.11 = f32[24,128]{1,0:T(8,128)} copy(f32[24,128]{1,0:T(8,128)S(1)} %get-tuple-element.5) | data formatting | bytes 24576
Async XLA Ops:
  2.0 0.7 %copy-start = (f32[24,128]{1,0:T(8,128)S(1)}, f32[24,128]{1,0:T(8,128)}, u32[]{:S(2)}) copy-start(f32[24,128]{1,0:T(8,128)} %right_hbm.1) | copy-start | bytes 36868
where the time goes:
time: 54.9 us; the launch traced here: 54.6 us
  Pallas kernels  50.7 us (92%)
  local copies, waits for them, and re-layouts  2.67 us (5%)
  between operations  1.29 us (2%)
    pallas_call x1, Pallas kernels, per_device(): pl.pallas_call(functools.partial(kernel, n_slab, n_sub), out_shape=(jax.S...  50.7 us
    unnamed x5, local copies, waits for them, and re-layouts  2.67 us

commit v1 on v0

v1 whole, which is shorter than its diff:
```python
import functools

import jax
import jax.numpy as jnp
from jax import lax
from jax.experimental import pallas as pl
from jax.experimental.pallas import tpu as pltpu
from jax.sharding import PartitionSpec as P

ITERS = 4
NB_DEV = 12
LANES = 128
SUMS = 3
MESH = pl.DeviceIdType.MESH


def round_up(size, unit):
    return -(-size // unit) * unit


def divisor(size, *wanted):
    return next(g for g in (*wanted, 1) if size % g == 0)


def kernel(
    n_slab,
    n_sub,
    values_hbm,
    ids_hbm,
    counts_hbm,
    right_hbm,
    solution_ref,
    residual_ref,
    values,
    wid,
    selector,
    terms,
    squares,
    cols,
    rows_ref,
    first_out,
    first_in,
    part_out,
    part_in,
    field_out,
    field_in,
    scal,
    ids_smem,
    counts_smem,
    right_ref,
    small_sem,
    load_sem,
    first_send,
    first_recv,
    part_send,
    part_recv,
    field_send,
    field_recv,
    scal_send,
    scal_recv,
):
    tiles, coupled, rows, block = values.shape
    halves = block // LANES
    held = NB_DEV * halves
    n = n_slab * n_sub
    window = 3 * n_sub * held
    n_terms = terms.shape[0]
    f32 = jnp.float32
    slab = lax.axis_index("slab")
    sub = lax.axis_index("sub")
    me = slab * n_sub + sub

    kept = slab + 1 - 2 * lax.rem(slab, 2)
    own_rel = kept - slab + 1
    beyond = 2 * slab - kept
    far_rel = slab - kept + 1
    far_out = 3 * slab - 2 * kept
    far_in = 2 * kept - slab
    sends_far = jnp.logical_and(beyond >= 0, beyond < n_slab)
    takes_far = jnp.logical_and(far_in >= 0, far_in < n_slab)

    small = [
        pltpu.make_async_copy(src, dst, small_sem.at[i])
        for i, (src, dst) in enumerate(
            ((ids_hbm, ids_smem), (counts_hbm, counts_smem), (right_hbm, right_ref))
        )
    ]
    for copy in small:
        copy.start()
    loads = load_sem.shape[0]
    group = tiles // loads

    def load(g):
        part = pl.ds(g * group, group)
        return pltpu.make_async_copy(values_hbm.at[part], values.at[part], load_sem.at[g])

    for g in range(loads):
        load(g).start()

    def other(j):
        target = lax.rem(me + j, n)
        return (lax.div(target, n_sub), lax.rem(target, n_sub))

    barrier = pltpu.get_barrier_semaphore()

    @pl.loop(1, n)
    def _(j):
        pl.semaphore_signal(barrier, inc=1, device_id=other(j), device_id_type=MESH)

    n_used = tiles * coupled * halves
    if n_terms > n_used:
        terms[n_used:] = jnp.zeros((n_terms - n_used, LANES), f32)
        squares[n_used:] = jnp.zeros((n_terms - n_used, LANES), f32)

    @pl.when(jnp.logical_not(takes_far))
    def _():
        for ref in (first_in, *part_in):
            ref[2 * n_sub :] = jnp.zeros((n_sub,) + ref.shape[1:], f32)

    @pl.when(jnp.logical_not(sends_far))
    def _():
        blank = pl.ds(pl.multiple_of(far_rel * n_sub * held, 8), n_sub * held)
        for ref in field_in:
            ref[blank, :] = jnp.zeros((n_sub * held, LANES), f32)

    for copy in small:
        copy.wait()

    base = (slab - 1) * n_sub * NB_DEV
    lane = lax.broadcasted_iota(jnp.int32, (1, n_terms), 1)
    lane_tile = lane % tiles
    lane_k = lane // (halves * tiles)
    lane_h = (lane // tiles) % halves
    place = jnp.full((1, n_terms), -1, jnp.int32)
    for t in range(tiles):
        for k in range(coupled):
            at = jnp.clip((ids_smem[t, k] - base) * halves, 0, window - halves)
            wid[t, k] = at
            place = jnp.where(jnp.logical_and(lane_tile == t, lane_k == k), at + lane_h, place)
    selector[...] = (
        lax.broadcasted_iota(jnp.int32, (window, n_terms), 0) == place
    ).astype(f32).astype(jnp.bfloat16)

    def live(t):
        return jnp.where(t < counts_smem[0, 0], 1.0, 0.0).astype(f32)

    eye = (
        lax.broadcasted_iota(jnp.int32, (rows, LANES), 0)
        == lax.broadcasted_iota(jnp.int32, (rows, LANES), 1)
    ).astype(f32)

    def half(h):
        return slice(h * LANES, (h + 1) * LANES)

    def term_row(k, h, t):
        return pl.ds((k * halves + h) * tiles + t, 1)

    @pl.loop(0, tiles // group)
    def _(g):
        for i in range(group):
            t = g * group + i
            alive = right_ref[pl.ds(t, 1), :] * live(t)
            residual_ref[pl.ds(t, 1), :] = alive
            cols[t] = jnp.broadcast_to(
                jnp.sum(eye * alive, axis=1, keepdims=True), (rows, LANES)
            )

    def scatter(ref):
        full = ref[...]
        high = full.astype(jnp.bfloat16)
        low = (full - high.astype(f32)).astype(jnp.bfloat16)
        spread = jnp.dot(
            selector[...], jnp.concatenate([high, low], axis=1), preferred_element_type=f32
        )
        return (spread[:, :LANES] + spread[:, LANES:]).reshape(3 * n_sub, held, LANES)

    def mates(act):
        for step in range(1, n_sub):
            act(step)

    def remote(src, dst, send, recv, device):
        return pltpu.make_async_remote_copy(
            src_ref=src, dst_ref=dst, send_sem=send, recv_sem=recv, device_id=device, device_id_type=MESH
        )

    def part_start(out_ref, in_ref, send, recv):
        def one(pos, rel, to_slab, step):
            target = lax.rem(sub + step, n_sub)
            remote(
                out_ref.at[rel * n_sub + target],
                in_ref.at[pos * n_sub + step],
                send.at[pos // 2],
                recv.at[pos // 2],
                (to_slab, target),
            ).start()

        @pl.when(sends_far)
        def _():
            for step in range(n_sub):
                one(2, far_rel, far_out, step)

        for step in range(n_sub):
            one(0, 1, kept, step)
        mates(lambda step: one(1, own_rel, slab, step))
        in_ref[n_sub] = out_ref[own_rel * n_sub + sub]

    def field_start(src, in_ref, send, recv):
        def one(sem, rel, to_slab, step):
            target = lax.rem(sub + step, n_sub)
            at = pl.multiple_of((rel * n_sub + sub) * held, 8)
            remote(
                src, in_ref.at[pl.ds(at, held)], send.at[sem], recv.at[sem], (to_slab, target)
            ).start()

        @pl.when(takes_far)
        def _():
            for step in range(n_sub):
                one(1, kept - far_in + 1, far_in, step)

        for step in range(n_sub):
            one(0, 1, kept, step)
        mates(lambda step: one(0, own_rel, slab, step))

    def group_wait(ref, per, sem, near, far_too, recv):
        def wait(i, count):
            size = ref.at[pl.ds(0, count * per)]
            copy = remote(size, size, sem.at[i], sem.at[i], (kept, sub))
            copy.wait_recv() if recv else copy.wait_send()

        wait(0, near)
        pl.when(far_too)(lambda: wait(1, n_sub))

    near = 2 * n_sub - 1

    def scal_copy(it, j):
        row = scal.at[it, pl.ds(me, 1)]
        return remote(row, row, scal_send.at[it], scal_recv.at[it], other(j))

    def scal_start(it, row):
        scal[it, pl.ds(me, 1)] = row

        @pl.loop(1, n)
        def _(j):
            scal_copy(it, j).start()

    def scal_all(it):
        rest = scal.at[it, pl.ds(0, n - 1)]
        return remote(rest, rest, scal_send.at[it], scal_recv.at[it], other(1))

    def total(x):
        return jnp.sum(jnp.sum(x, axis=0, keepdims=True), axis=1, keepdims=True)

    lane_row = lax.broadcasted_iota(jnp.int32, (1, LANES), 1)

    def pack(parts):
        row = jnp.zeros((1, LANES), f32)
        for i, x in enumerate(parts):
            row = jnp.where(lane_row == i, total(x), row)
        return row

    def unpack(it, count):
        row = jnp.sum(scal[it], axis=0, keepdims=True)
        return [
            jnp.sum(jnp.where(lane_row == i, row, 0.0), axis=1, keepdims=True)
            for i in range(count)
        ]

    @pl.loop(0, loads)
    def _(g):
        load(g).wait()
        for i in range(group):
            t = g * group + i
            alive = live(t)
            right = cols[t]
            for k in range(coupled):
                for h in range(halves):
                    a = values[t, k, :, half(h)]
                    terms[term_row(k, h, t), :] = jnp.sum(a * right, axis=0, keepdims=True)
                    squares[term_row(k, h, t), :] = (
                        jnp.sum(a * a, axis=0, keepdims=True) * alive
                    )

    for i, ref in enumerate((terms, squares)):
        first_out[:, i] = scatter(ref)
    pl.semaphore_wait(barrier, n - 1)
    part_start(first_out, first_in, first_send, first_recv)
    group_wait(first_in, 1, first_recv, near, takes_far, True)
    sums = jnp.sum(first_in[...], axis=0)
    normal_res = sums[0]
    jacobi = 1.0 / (1.0 + sums[1])

    def own_rows(ref):
        return ref[pl.ds(pl.multiple_of((n_sub + sub) * held, 8), held), :]

    def send_field(it, field):
        field_out[it] = field
        at = pl.multiple_of((own_rel * n_sub + sub) * held, 8)
        field_start(field_out.at[it], field_in[it], field_send.at[it], field_recv.at[it])
        field_in[it][pl.ds(at, held), :] = field

    scaled = jacobi * normal_res
    kept_dir = scaled
    field = scaled
    send_field(0, field)
    scal_start(0, pack((normal_res * scaled,)))
    answer = jnp.zeros((held, LANES), f32)
    for it in range(ITERS):
        last = it == ITERS - 1
        fields = field_in[it]
        group_wait(fields, held, field_recv.at[it], near, sends_far, True)

        def forward(t):
            alive = live(t)
            m = None
            for k in range(coupled):
                for h in range(halves):
                    picked = fields[pl.ds(wid[t, k] + h, 1), :] * alive
                    product = values[t, k, :, half(h)] * picked
                    m = product if m is None else m + product
            cols[t] = jnp.broadcast_to(jnp.sum(m, axis=1, keepdims=True), (rows, LANES))

        def backward(t):
            image = cols[t]
            for k in range(coupled):
                for h in range(halves):
                    terms[term_row(k, h, t), :] = jnp.sum(
                        values[t, k, :, half(h)] * image, axis=0, keepdims=True
                    )

        step = divisor(tiles, 4, 3, 2)
        for i in range(step):
            forward(i)

        @pl.loop(1, tiles // step)
        def _(g):
            if not last:
                for i in range(step):
                    backward((g - 1) * step + i)
            for i in range(step):
                forward(g * step + i)

        if not last:
            for i in range(step):
                backward(tiles - step + i)
            part_out[it] = scatter(terms)
            part_start(part_out.at[it], part_in[it], part_send.at[it], part_recv.at[it])

        @pl.loop(0, tiles, unroll=4)
        def _(t):
            rows_ref[pl.ds(t, 1), :] = jnp.sum(cols[t] * eye, axis=0, keepdims=True)

        field_own = own_rows(fields)
        scal_all(it).wait_recv()
        if it == 0:
            (rho,) = unpack(0, 1)
            scaled_own = field_own
            direction = field_own
            scaled_image = rows_ref[...]
            image = scaled_image
        else:
            curve, cross, square = unpack(it, SUMS)
            step_size = rho / curve
            rho_next = rho - 2.0 * step_size * cross + step_size * step_size * square
            beta = rho_next / rho
            rho = rho_next
            answer = answer + step_size * direction
            residual_ref[...] = residual_ref[...] - step_size * image
            scaled = scaled - step_size * field
            kept_dir = scaled + beta * kept_dir
            scaled_own = scaled_own - step_size * field_own
            direction = scaled_own + beta * direction
            scaled_image = scaled_image - step_size * rows_ref[...]
            image = scaled_image + beta * image

        if last:
            scal_start(ITERS, pack((image * image,)))
        else:
            group_wait(part_in[it], 1, part_recv.at[it], near, takes_far, True)
            spread = jnp.sum(part_in[it][...], axis=0)
            if it == 0:
                scaled_back = spread
                back = spread
            else:
                scaled_back = scaled_back - step_size * spread
                back = scaled_back + beta * back
            field = jacobi * back
            send_field(it + 1, field)
            scal_start(it + 1, pack((kept_dir * back, scaled * back, back * field)))

    scal_all(ITERS).wait_recv()
    (curve,) = unpack(ITERS, 1)
    step_size = rho / curve
    answer = answer + step_size * direction
    residual_ref[...] = residual_ref[...] - step_size * image
    rows_ref[:held] = answer
    for h in range(halves):
        solution_ref[:, half(h)] = rows_ref[pl.ds(h, NB_DEV, stride=halves), :]

    group_wait(first_in, 1, first_send, near, sends_far, False)
    for it in range(ITERS):
        group_wait(field_in[it], held, field_send.at[it], near, takes_far, False)
        if it < ITERS - 1:
            group_wait(part_in[it], 1, part_send.at[it], near, sends_far, False)
    for it in range(ITERS + 1):
        scal_all(it).wait_send()


def per_device(n_slab, n_sub, values, block_ids, tile_counts, right_side):
    tiles, coupled, rows, block = values.shape
    halves = block // LANES
    held = NB_DEV * halves
    n = n_slab * n_sub
    slots = 3 * n_sub
    window = slots * held
    n_terms = round_up(tiles * coupled * halves, LANES)
    loads = tiles // divisor(tiles, 4, 3, 2)
    f32 = jnp.float32
    vmem = pltpu.VMEM
    dma = pltpu.SemaphoreType.DMA
    whole = pl.BlockSpec(memory_space=pltpu.VMEM)
    return pl.pallas_call(
        functools.partial(kernel, n_slab, n_sub),
        out_shape=(
            jax.ShapeDtypeStruct((NB_DEV, block), f32),
            jax.ShapeDtypeStruct((tiles, rows), f32),
        ),
        in_specs=[pl.BlockSpec(memory_space=pl.ANY)] * 4,
        out_specs=(whole, whole),
        scratch_shapes=[
            vmem(values.shape, f32),
            pltpu.SMEM((tiles, coupled), jnp.int32),
            vmem((window, n_terms), jnp.bfloat16),
            vmem((n_terms, LANES), f32),
            vmem((n_terms, LANES), f32),
            vmem((tiles, rows, LANES), f32),
            vmem((tiles, LANES), f32),
            vmem((slots, 2, held, LANES), f32),
            vmem((slots, 2, held, LANES), f32),
            vmem((ITERS - 1, slots, held, LANES), f32),
            [vmem((slots, held, LANES), f32)] * (ITERS - 1),
            vmem((ITERS, held, LANES), f32),
            [vmem((window, LANES), f32)] * ITERS,
            vmem((ITERS + 1, n, LANES), f32),
            pltpu.SMEM((tiles, coupled), jnp.int32),
            pltpu.SMEM((1, 1), jnp.int32),
            vmem((tiles, rows), f32),
            dma((3,)),
            dma((loads,)),
            dma((2,)),
            dma((2,)),
            dma((ITERS - 1, 2)),
            dma((ITERS - 1, 2)),
            dma((ITERS, 2)),
            dma((ITERS, 2)),
            dma((ITERS + 1,)),
            dma((ITERS + 1,)),
        ],
        compiler_params=pltpu.CompilerParams(
            collective_id=0, has_side_effects=True, vmem_limit_bytes=48 * 1024 * 1024
        ),
    )(values, block_ids, tile_counts, right_side)


def solution(mesh):
    in_specs = (
        P(("slab", "sub"), None, None, None),
        P(("slab", "sub"), None),
        P("slab", "sub"),
        P(("slab", "sub"), None),
    )
    out_specs = (P(("slab", "sub"), None), P(("slab", "sub"), None))
    return jax.shard_map(
        functools.partial(per_device, mesh.shape["slab"], mesh.shape["sub"]),
        mesh=mesh,
        in_specs=in_specs,
        out_specs=out_specs,
        check_vma=False,
    )
```

time: 54.9 us -> 52.7 us (0.960)
  Pallas kernels: 50.7 us -> 48.5 us
    pallas_call x1, Pallas kernels: 50.7 us -> 48.5 us  [per_device(): pl.pallas_call(functools.partial(kernel, n_slab, n_sub), out_shape=(jax.S...]
where the time goes in v1:
time: 52.7 us; the launch traced here: 52.5 us
  Pallas kernels  48.5 us (92%)
  local copies, waits for them, and re-layouts  2.67 us (5%)
  between operations  1.29 us (2%)
    pallas_call x1, Pallas kernels, per_device(): pl.pallas_call(functools.partial(kernel, n_slab, n_sub), out_shape=(jax.S...  48.5 us
    unnamed x5, local copies, waits for them, and re-layouts  2.67 us

profile of v1, /device:TPU:0, one launch (start us, length us, event | category | flops | bytes accessed | tf_op | source)
XLA Modules:
  0.0 52.5 jit_solution(6464365732675147855)
XLA Ops:
  1.3 0.8 %copy.6.ids_hbm = s32[24,2]{1,0:T(8,128)S(1)} copy(s32[24,2]{0,1:T(2,128)} %param.5) | data formatting | bytes 384 | tf_op args[1]
  2.0 0.0 copy-start
  2.0 0.7 %copy-done = f32[24,128]{1,0:T(8,128)S(1)} copy-done((f32[24,128]{1,0:T(8,128)S(1)}, f32[24,128]{1,0:T(8,128)}, u32[]{:S(2)}) %copy-start) | copy-done | bytes 12312
  2.7 48.5 %shard_map.59 = (f32[12,256]{1,0:T(8,128)S(1)}, f32[24,128]{1,0:T(8,128)S(1)}) custom-call(f32[24,2,128,256]{3,2,1,0:T(8,128)} %values_hbm.1, s32[24,2]{1,0:T(8,128)S(1)} %copy.6.ids_hbm, s32[1,1]{1,0:T(1,128)S(6)} %copy.9.counts_hbm, f32[24,128]{1,0:T(8,128)S(1)} %copy-done), custom_call_target="tpu_custom_call" | custom-call | tf_op jit(solution)/shard_map/pallas_call | solution.py:421
  51.3 0.6 %copy.10 = f32[12,256]{1,0:T(8,128)} copy(f32[12,256]{1,0:T(8,128)S(1)} %get-tuple-element.4) | data formatting | bytes 24576
  51.9 0.6 %copy.11 = f32[24,128]{1,0:T(8,128)} copy(f32[24,128]{1,0:T(8,128)S(1)} %get-tuple-element.5) | data formatting | bytes 24576
Async XLA Ops:
  2.0 0.7 %copy-start = (f32[24,128]{1,0:T(8,128)S(1)}, f32[24,128]{1,0:T(8,128)}, u32[]{:S(2)}) copy-start(f32[24,128]{1,0:T(8,128)} %right_hbm.1) | copy-start | bytes 36868

commit v2 on v1

--- a/solution.py
+++ b/solution.py
@@ -11,6 +11,7 @@
 NB_DEV = 12
 LANES = 128
 SUMS = 3
+STEP = 4
 MESH = pl.DeviceIdType.MESH
 
 
@@ -58,6 +59,7 @@
     field_recv,
     scal_send,
     scal_recv,
+    hello,
 ):
     tiles, coupled, rows, block = values.shape
     halves = block // LANES
@@ -103,9 +105,30 @@
 
     barrier = pltpu.get_barrier_semaphore()
 
-    @pl.loop(1, n)
-    def _(j):
-        pl.semaphore_signal(barrier, inc=1, device_id=other(j), device_id_type=MESH)
+    def greet(slot, to_slab, target):
+        pl.semaphore_signal(slot, inc=1, device_id=(to_slab, target), device_id_type=MESH)
+
+    for exists, to_slab in ((sends_far, far_out), (takes_far, far_in)):
+
+        @pl.when(exists)
+        def _():
+            for step in range(n_sub):
+                greet(barrier, to_slab, lax.rem(sub + step, n_sub))
+
+    for step in range(n_sub):
+        greet(barrier, kept, lax.rem(sub + step, n_sub))
+    for step in range(1, n_sub):
+        greet(barrier, slab, lax.rem(sub + step, n_sub))
+
+    fars = sends_far.astype(jnp.int32) + takes_far.astype(jnp.int32)
+    rounds = hello.shape[0]
+
+    def pass_on(r):
+        if r > 0:
+            pl.semaphore_wait(hello.at[r - 1], fars)
+        if r < rounds:
+            pl.when(sends_far)(lambda: greet(hello.at[r], far_out, sub))
+            pl.when(takes_far)(lambda: greet(hello.at[r], far_in, sub))
 
     n_used = tiles * coupled * halves
     if n_terms > n_used:
@@ -134,7 +157,7 @@
     place = jnp.full((1, n_terms), -1, jnp.int32)
     for t in range(tiles):
         for k in range(coupled):
-            at = jnp.clip((ids_smem[t, k] - base) * halves, 0, window - halves)
+            at = jnp.clip((ids_smem[k, t] - base) * halves, 0, window - halves)
             wid[t, k] = at
             place = jnp.where(jnp.logical_and(lane_tile == t, lane_k == k), at + lane_h, place)
     selector[...] = (
@@ -239,7 +262,7 @@
     def scal_start(it, row):
         scal[it, pl.ds(me, 1)] = row
 
-        @pl.loop(1, n)
+        @pl.loop(1, n, unroll=min(n - 1, 31))
         def _(j):
             scal_copy(it, j).start()
 
@@ -264,6 +287,10 @@
             jnp.sum(jnp.where(lane_row == i, row, 0.0), axis=1, keepdims=True)
             for i in range(count)
         ]
+
+    def turn(x):
+        rest = jnp.zeros((LANES - tiles, LANES), f32)
+        return jnp.concatenate([x, rest], axis=0).T
 
     @pl.loop(0, loads)
     def _(g):
@@ -282,8 +309,9 @@
 
     for i, ref in enumerate((terms, squares)):
         first_out[:, i] = scatter(ref)
-    pl.semaphore_wait(barrier, n - 1)
+    pl.semaphore_wait(barrier, 2 * n_sub - 1 + n_sub * fars)
     part_start(first_out, first_in, first_send, first_recv)
+    pass_on(0)
     group_wait(first_in, 1, first_recv, near, takes_far, True)
     sums = jnp.sum(first_in[...], axis=0)
     normal_res = sums[0]
@@ -302,14 +330,15 @@
     kept_dir = scaled
     field = scaled
     send_field(0, field)
-    scal_start(0, pack((normal_res * scaled,)))
+    pass_on(1)
+    rho_part = normal_res * scaled
     answer = jnp.zeros((held, LANES), f32)
     for it in range(ITERS):
         last = it == ITERS - 1
         fields = field_in[it]
         group_wait(fields, held, field_recv.at[it], near, sends_far, True)
 
-        def forward(t):
+        def reduced(t):
             alive = live(t)
             m = None
             for k in range(coupled):
@@ -317,7 +346,10 @@
                     picked = fields[pl.ds(wid[t, k] + h, 1), :] * alive
                     product = values[t, k, :, half(h)] * picked
                     m = product if m is None else m + product
-            cols[t] = jnp.broadcast_to(jnp.sum(m, axis=1, keepdims=True), (rows, LANES))
+            return jnp.broadcast_to(jnp.sum(m, axis=1, keepdims=True), (rows, LANES))
+
+        def forward(t):
+            cols[t] = reduced(t)
 
         def backward(t):
             image = cols[t]
@@ -327,38 +359,71 @@
                         values[t, k, :, half(h)] * image, axis=0, keepdims=True
                     )
 
-        step = divisor(tiles, 4, 3, 2)
-        for i in range(step):
-            forward(i)
-
-        @pl.loop(1, tiles // step)
-        def _(g):
-            if not last:
+        step = divisor(tiles, STEP, 3, 2)
+        if last:
+
+            def turned_step(g, turned):
+                for i in range(step):
+                    t = g * step + i
+                    turned = jnp.where(lane_row == t, reduced(t), turned)
+                return turned
+
+            image_t = turn(image)
+            turned = turn(scaled_image)
+            pushed = lax.fori_loop(0, tiles // step, turned_step, jnp.zeros((rows, LANES), f32))
+        else:
+            for i in range(step):
+                forward(i)
+
+            @pl.loop(1, tiles // step)
+            def _(g):
                 for i in range(step):
                     backward((g - 1) * step + i)
-            for i in range(step):
-                forward(g * step + i)
-
-        if not last:
+                for i in range(step):
+                    forward(g * step + i)
+
             for i in range(step):
                 backward(tiles - step + i)
             part_out[it] = scatter(terms)
             part_start(part_out.at[it], part_in[it], part_send.at[it], part_recv.at[it])
 
-        @pl.loop(0, tiles, unroll=4)
-        def _(t):
-            rows_ref[pl.ds(t, 1), :] = jnp.sum(cols[t] * eye, axis=0, keepdims=True)
+            @pl.loop(0, tiles, unroll=4)
+            def _(t):
+                rows_ref[pl.ds(t, 1), :] = jnp.sum(cols[t] * eye, axis=0, keepdims=True)
 
         field_own = own_rows(fields)
-        scal_all(it).wait_recv()
         if it == 0:
-            (rho,) = unpack(0, 1)
+            for r in range(2, rounds + 1):
+                pass_on(r)
             scaled_own = field_own
             direction = field_own
             scaled_image = rows_ref[...]
             image = scaled_image
+        elif last:
+            scal_all(ITERS).wait_recv()
+            curve, cross = unpack(ITERS, 2)
+            step_size = rho / curve
+            turned = turned - step_size * pushed
+            scal_start(
+                it, pack((turned * turned, turned * image_t, image_t * image_t))
+            )
+            answer = answer + step_size * direction
+            residual = residual_ref[...] - step_size * image
+            scaled_own = scaled_own - step_size * field_own
+            scaled_image = turned.T[:tiles]
+            scal_all(it - 1).wait_recv()
+            (square,) = unpack(it - 1, 1)
+            rho_next = rho - 2.0 * step_size * cross + step_size * step_size * square
+            beta = rho_next / rho
+            rho = rho_next
+            direction = scaled_own + beta * direction
+            image = scaled_image + beta * image
         else:
-            curve, cross, square = unpack(it, SUMS)
+            scal_all(it - 1).wait_recv()
+            if it == 1:
+                curve, cross, square, rho = unpack(it - 1, SUMS + 1)
+            else:
+                curve, cross, square = unpack(it - 1, SUMS)
             step_size = rho / curve
             rho_next = rho - 2.0 * step_size * cross + step_size * step_size * square
             beta = rho_next / rho
@@ -372,9 +437,9 @@
             scaled_image = scaled_image - step_size * rows_ref[...]
             image = scaled_image + beta * image
 
-        if last:
-            scal_start(ITERS, pack((image * image,)))
-        else:
+        if it == ITERS - 2:
+            scal_start(ITERS, pack((image * image, scaled_image * image)))
+        if not last:
             group_wait(part_in[it], 1, part_recv.at[it], near, takes_far, True)
             spread = jnp.sum(part_in[it][...], axis=0)
             if it == 0:
@@ -385,13 +450,16 @@
                 back = scaled_back + beta * back
             field = jacobi * back
             send_field(it + 1, field)
-            scal_start(it + 1, pack((kept_dir * back, scaled * back, back * field)))
-
-    scal_all(ITERS).wait_recv()
-    (curve,) = unpack(ITERS, 1)
-    step_size = rho / curve
+            parts = (kept_dir * back, scaled * back, back * field)
+            if it == 0:
+                parts = parts + (rho_part,)
+            scal_start(it, pack(parts[2:] if it == ITERS - 2 else parts))
+
+    scal_all(ITERS - 1).wait_recv()
+    new, mixed, old = unpack(ITERS - 1, SUMS)
+    step_size = rho / (new + 2.0 * beta * mixed + beta * beta * old)
     answer = answer + step_size * direction
-    residual_ref[...] = residual_ref[...] - step_size * image
+    residual_ref[...] = residual - step_size * image
     rows_ref[:held] = answer
     for h in range(halves):
         solution_ref[:, half(h)] = rows_ref[pl.ds(h, NB_DEV, stride=halves), :]
@@ -424,7 +492,7 @@
             jax.ShapeDtypeStruct((NB_DEV, block), f32),
             jax.ShapeDtypeStruct((tiles, rows), f32),
         ),
-        in_specs=[pl.BlockSpec(memory_space=pl.ANY)] * 4,
+        in_specs=[pl.BlockSpec(memory_space=pltpu.HBM)] * 4,
         out_specs=(whole, whole),
         scratch_shapes=[
             vmem(values.shape, f32),
@@ -441,7 +509,7 @@
             vmem((ITERS, held, LANES), f32),
             [vmem((window, LANES), f32)] * ITERS,
             vmem((ITERS + 1, n, LANES), f32),
-            pltpu.SMEM((tiles, coupled), jnp.int32),
+            pltpu.SMEM((coupled, tiles), jnp.int32),
             pltpu.SMEM((1, 1), jnp.int32),
             vmem((tiles, rows), f32),
             dma((3,)),
@@ -454,11 +522,12 @@
             dma((ITERS, 2)),
             dma((ITERS + 1,)),
             dma((ITERS + 1,)),
+            pltpu.SemaphoreType.REGULAR((max(1, n_slab // 2 - 1),)),
         ],
         compiler_params=pltpu.CompilerParams(
             collective_id=0, has_side_effects=True, vmem_limit_bytes=48 * 1024 * 1024
         ),
-    )(values, block_ids, tile_counts, right_side)
+    )(values, block_ids.T, tile_counts, right_side)
 
 
 def solution(mesh):

time: 52.7 us -> 52.5 us (level)
    unnamed x5 -> x6, local copies, waits for them, and re-layouts: 2.67 us -> 2.59 us
where the time goes in v2:
time: 52.5 us; the launch traced here: 52.3 us
  Pallas kernels  48.4 us (92%)
  local copies, waits for them, and re-layouts  2.59 us (5%)
  between operations  1.29 us (2%)
    pallas_call x1, Pallas kernels, per_device(): pl.pallas_call(functools.partial(kernel, n_slab, n_sub), out_shape=(jax.S...  48.4 us
    unnamed x6, local copies, waits for them, and re-layouts  2.59 us

profile of v2, /device:TPU:0, one launch (start us, length us, event | category | flops | bytes accessed | tf_op | source)
XLA Modules:
  0.0 52.3 jit_solution(138539742889041063)
XLA Ops:
  1.3 0.0 copy-start
  1.3 0.7 %copy-done = f32[24,128]{1,0:T(8,128)S(1)} copy-done((f32[24,128]{1,0:T(8,128)S(1)}, f32[24,128]{1,0:T(8,128)}, u32[]{:S(2)}) %copy-start) | copy-done | bytes 12312
  2.0 0.0 copy-start.1
  2.0 0.7 %copy-done.1 = s32[24,2]{0,1:T(2,128)S(1)} copy-done((s32[24,2]{0,1:T(2,128)S(1)}, s32[24,2]{0,1:T(2,128)}, u32[]{:S(2)}) %copy-start.1) | copy-done | bytes 216
  2.7 48.4 %shard_map.59 = (f32[12,256]{1,0:T(8,128)S(1)}, f32[24,128]{1,0:T(8,128)S(1)}) custom-call(f32[24,2,128,256]{3,2,1,0:T(8,128)} %values_hbm.1, s32[2,24]{1,0:T(2,128)S(1)} %bitcast.1, s32[1,1]{1,0:T(1,128)S(6)} %copy.8.counts_hbm, f32[24,128]{1,0:T(8,128)S(1)} %copy-done), custom_call_target="tpu_custom_call" | custom-call | tf_op jit(solution)/shard_map/pallas_call | solution.py:489
  51.1 0.6 %copy.9 = f32[12,256]{1,0:T(8,128)} copy(f32[12,256]{1,0:T(8,128)S(1)} %get-tuple-element.4) | data formatting | bytes 24576
  51.7 0.6 %copy.10 = f32[24,128]{1,0:T(8,128)} copy(f32[24,128]{1,0:T(8,128)S(1)} %get-tuple-element.5) | data formatting | bytes 24576
Async XLA Ops:
  1.3 0.7 %copy-start = (f32[24,128]{1,0:T(8,128)S(1)}, f32[24,128]{1,0:T(8,128)}, u32[]{:S(2)}) copy-start(f32[24,128]{1,0:T(8,128)} %right_hbm.1) | copy-start | bytes 36868
  2.0 0.7 %copy-start.1 = (s32[24,2]{0,1:T(2,128)S(1)}, s32[24,2]{0,1:T(2,128)}, u32[]{:S(2)}) copy-start(s32[24,2]{0,1:T(2,128)} %param.5) | copy-start | bytes 580

commit v3 on v2

--- a/solution.py
+++ b/solution.py
@@ -11,7 +11,7 @@
 NB_DEV = 12
 LANES = 128
 SUMS = 3
-STEP = 4
+STEP = 12
 MESH = pl.DeviceIdType.MESH
 
 
@@ -60,6 +60,12 @@
     scal_send,
     scal_recv,
     hello,
+    jacobi,
+    scaled,
+    kept_dir,
+    scaled_back,
+    back,
+    rho_row,
 ):
     tiles, coupled, rows, block = values.shape
     halves = block // LANES
@@ -71,6 +77,11 @@
     slab = lax.axis_index("slab")
     sub = lax.axis_index("sub")
     me = slab * n_sub + sub
+    pairs = n_sub // 2
+    span = 2 * held
+    pair = lax.div(sub, 2)
+    sums_here = lax.rem(sub, 2) == 1
+    rests_here = lax.rem(sub, 2) == 0
 
     kept = slab + 1 - 2 * lax.rem(slab, 2)
     own_rel = kept - slab + 1
@@ -195,11 +206,7 @@
         spread = jnp.dot(
             selector[...], jnp.concatenate([high, low], axis=1), preferred_element_type=f32
         )
-        return (spread[:, :LANES] + spread[:, LANES:]).reshape(3 * n_sub, held, LANES)
-
-    def mates(act):
-        for step in range(1, n_sub):
-            act(step)
+        return (spread[:, :LANES] + spread[:, LANES:]).reshape(3 * pairs, span, LANES)
 
     def remote(src, dst, send, recv, device):
         return pltpu.make_async_remote_copy(
@@ -208,67 +215,95 @@
 
     def part_start(out_ref, in_ref, send, recv):
         def one(pos, rel, to_slab, step):
-            target = lax.rem(sub + step, n_sub)
+            target = lax.rem(pair + step, pairs)
             remote(
-                out_ref.at[rel * n_sub + target],
-                in_ref.at[pos * n_sub + step],
+                out_ref.at[rel * pairs + target],
+                in_ref.at[pos * n_sub + sub],
                 send.at[pos // 2],
                 recv.at[pos // 2],
-                (to_slab, target),
+                (to_slab, 2 * target + 1),
             ).start()
 
         @pl.when(sends_far)
         def _():
-            for step in range(n_sub):
+            for step in range(1, pairs + 1):
                 one(2, far_rel, far_out, step)
 
-        for step in range(n_sub):
+        for step in range(1, pairs + 1):
             one(0, 1, kept, step)
-        mates(lambda step: one(1, own_rel, slab, step))
-        in_ref[n_sub] = out_ref[own_rel * n_sub + sub]
+        for step in range(1, pairs):
+            one(1, own_rel, slab, step)
+        pl.when(rests_here)(lambda: one(1, own_rel, slab, pairs))
+
+        @pl.when(sums_here)
+        def _():
+            in_ref[n_sub + sub] = out_ref[own_rel * pairs + pair]
 
     def field_start(src, in_ref, send, recv):
-        def one(sem, rel, to_slab, step):
-            target = lax.rem(sub + step, n_sub)
-            at = pl.multiple_of((rel * n_sub + sub) * held, 8)
+        def one(sem, rel, to_slab, step, core):
+            target = 2 * lax.rem(pair + step, pairs) + core
+            at = pl.multiple_of((rel * pairs + pair) * span, 8)
             remote(
-                src, in_ref.at[pl.ds(at, held)], send.at[sem], recv.at[sem], (to_slab, target)
+                src, in_ref.at[pl.ds(at, span)], send.at[sem], recv.at[sem], (to_slab, target)
             ).start()
+
+        order = [(step, core) for core in range(2) for step in range(1, pairs + 1)]
 
         @pl.when(takes_far)
         def _():
-            for step in range(n_sub):
-                one(1, kept - far_in + 1, far_in, step)
-
-        for step in range(n_sub):
-            one(0, 1, kept, step)
-        mates(lambda step: one(0, own_rel, slab, step))
-
-    def group_wait(ref, per, sem, near, far_too, recv):
+            for step, core in order:
+                one(1, kept - far_in + 1, far_in, step, core)
+
+        for step, core in order:
+            one(0, 1, kept, step, core)
+        for step, core in order:
+            if (step, core) != (pairs, 1):
+                one(0, own_rel, slab, step, core)
+
+    def group_wait(ref, per, sem, counts, far_too, recv):
         def wait(i, count):
             size = ref.at[pl.ds(0, count * per)]
             copy = remote(size, size, sem.at[i], sem.at[i], (kept, sub))
             copy.wait_recv() if recv else copy.wait_send()
 
-        wait(0, near)
-        pl.when(far_too)(lambda: wait(1, n_sub))
-
-    near = 2 * n_sub - 1
+        near, far = counts
+        if isinstance(near, tuple):
+            pl.when(sums_here)(lambda: wait(0, near[0]))
+            pl.when(rests_here)(lambda: wait(0, near[1]))
+        else:
+            wait(0, near)
+        pl.when(far_too)(lambda: wait(1, far))
+
+    by_pair = ((2 * pairs - 1, 2 * pairs), pairs)
+    by_sub = (2 * n_sub - 1, n_sub)
+
+    summing = slab * pairs + pair
+
+    def from_all(it):
+        return it >= ITERS - 1
 
     def scal_copy(it, j):
-        row = scal.at[it, pl.ds(me, 1)]
+        row = scal.at[it, pl.ds(me if from_all(it) else summing, 1)]
         return remote(row, row, scal_send.at[it], scal_recv.at[it], other(j))
 
     def scal_start(it, row):
-        scal[it, pl.ds(me, 1)] = row
+        scal[it, pl.ds(me if from_all(it) else summing, 1)] = row
 
         @pl.loop(1, n, unroll=min(n - 1, 31))
         def _(j):
             scal_copy(it, j).start()
 
-    def scal_all(it):
-        rest = scal.at[it, pl.ds(0, n - 1)]
-        return remote(rest, rest, scal_send.at[it], scal_recv.at[it], other(1))
+    def scal_wait(it, count, recv):
+        rest = scal.at[it, pl.ds(0, count)]
+        copy = remote(rest, rest, scal_send.at[it], scal_recv.at[it], other(1))
+        copy.wait_recv() if recv else copy.wait_send()
+
+    def scal_take(it):
+        if from_all(it):
+            scal_wait(it, n - 1, True)
+        else:
+            pl.when(sums_here)(lambda: scal_wait(it, n // 2 - 1, True))
+            pl.when(rests_here)(lambda: scal_wait(it, n // 2, True))
 
     def total(x):
         return jnp.sum(jnp.sum(x, axis=0, keepdims=True), axis=1, keepdims=True)
@@ -282,7 +317,7 @@
         return row
 
     def unpack(it, count):
-        row = jnp.sum(scal[it], axis=0, keepdims=True)
+        row = jnp.sum(scal[it][: n if from_all(it) else n // 2], axis=0, keepdims=True)
         return [
             jnp.sum(jnp.where(lane_row == i, row, 0.0), axis=1, keepdims=True)
             for i in range(count)
@@ -312,31 +347,31 @@
     pl.semaphore_wait(barrier, 2 * n_sub - 1 + n_sub * fars)
     part_start(first_out, first_in, first_send, first_recv)
     pass_on(0)
-    group_wait(first_in, 1, first_recv, near, takes_far, True)
-    sums = jnp.sum(first_in[...], axis=0)
-    normal_res = sums[0]
-    jacobi = 1.0 / (1.0 + sums[1])
-
+    pass_on(1)
     def own_rows(ref):
         return ref[pl.ds(pl.multiple_of((n_sub + sub) * held, 8), held), :]
 
     def send_field(it, field):
         field_out[it] = field
-        at = pl.multiple_of((own_rel * n_sub + sub) * held, 8)
+        at = pl.multiple_of((own_rel * pairs + pair) * span, 8)
         field_start(field_out.at[it], field_in[it], field_send.at[it], field_recv.at[it])
-        field_in[it][pl.ds(at, held), :] = field
-
-    scaled = jacobi * normal_res
-    kept_dir = scaled
-    field = scaled
-    send_field(0, field)
-    pass_on(1)
-    rho_part = normal_res * scaled
+        field_in[it][pl.ds(at, span), :] = field
+
+    @pl.when(sums_here)
+    def _():
+        group_wait(first_in, 1, first_recv, by_sub, takes_far, True)
+        sums = jnp.sum(first_in[...], axis=0)
+        jacobi[...] = 1.0 / (1.0 + sums[1])
+        scaled[...] = jacobi[...] * sums[0]
+        kept_dir[...] = scaled[...]
+        send_field(0, scaled[...])
+        rho_row[...] = jnp.where(lane_row == SUMS, total(sums[0] * scaled[...]), 0.0)
+
     answer = jnp.zeros((held, LANES), f32)
     for it in range(ITERS):
         last = it == ITERS - 1
         fields = field_in[it]
-        group_wait(fields, held, field_recv.at[it], near, sends_far, True)
+        group_wait(fields, span, field_recv.at[it], by_pair, sends_far, True)
 
         def reduced(t):
             alive = live(t)
@@ -400,7 +435,7 @@
             scaled_image = rows_ref[...]
             image = scaled_image
         elif last:
-            scal_all(ITERS).wait_recv()
+            scal_take(ITERS)
             curve, cross = unpack(ITERS, 2)
             step_size = rho / curve
             turned = turned - step_size * pushed
@@ -411,7 +446,7 @@
             residual = residual_ref[...] - step_size * image
             scaled_own = scaled_own - step_size * field_own
             scaled_image = turned.T[:tiles]
-            scal_all(it - 1).wait_recv()
+            scal_take(it - 1)
             (square,) = unpack(it - 1, 1)
             rho_next = rho - 2.0 * step_size * cross + step_size * step_size * square
             beta = rho_next / rho
@@ -419,7 +454,7 @@
             direction = scaled_own + beta * direction
             image = scaled_image + beta * image
         else:
-            scal_all(it - 1).wait_recv()
+            scal_take(it - 1)
             if it == 1:
                 curve, cross, square, rho = unpack(it - 1, SUMS + 1)
             else:
@@ -430,8 +465,6 @@
             rho = rho_next
             answer = answer + step_size * direction
             residual_ref[...] = residual_ref[...] - step_size * image
-            scaled = scaled - step_size * field
-            kept_dir = scaled + beta * kept_dir
             scaled_own = scaled_own - step_size * field_own
             direction = scaled_own + beta * direction
             scaled_image = scaled_image - step_size * rows_ref[...]
@@ -440,22 +473,30 @@
         if it == ITERS - 2:
             scal_start(ITERS, pack((image * image, scaled_image * image)))
         if not last:
-            group_wait(part_in[it], 1, part_recv.at[it], near, takes_far, True)
-            spread = jnp.sum(part_in[it][...], axis=0)
-            if it == 0:
-                scaled_back = spread
-                back = spread
-            else:
-                scaled_back = scaled_back - step_size * spread
-                back = scaled_back + beta * back
-            field = jacobi * back
-            send_field(it + 1, field)
-            parts = (kept_dir * back, scaled * back, back * field)
-            if it == 0:
-                parts = parts + (rho_part,)
-            scal_start(it, pack(parts[2:] if it == ITERS - 2 else parts))
-
-    scal_all(ITERS - 1).wait_recv()
+
+            @pl.when(sums_here)
+            def _():
+                if it > 0:
+                    scaled[...] = scaled[...] - step_size * field_out[it]
+                    kept_dir[...] = scaled[...] + beta * kept_dir[...]
+                group_wait(part_in[it], 1, part_recv.at[it], by_sub, takes_far, True)
+                spread = jnp.sum(part_in[it][...], axis=0)
+                if it == 0:
+                    scaled_back[...] = spread
+                    back[...] = spread
+                else:
+                    scaled_back[...] = scaled_back[...] - step_size * spread
+                    back[...] = scaled_back[...] + beta * back[...]
+                field = jacobi[...] * back[...]
+                send_field(it + 1, field)
+                square = back[...] * field
+                if it == ITERS - 2:
+                    row = pack((square,))
+                else:
+                    row = pack((kept_dir[...] * back[...], scaled[...] * back[...], square))
+                scal_start(it, row + rho_row[...] if it == 0 else row)
+
+    scal_take(ITERS - 1)
     new, mixed, old = unpack(ITERS - 1, SUMS)
     step_size = rho / (new + 2.0 * beta * mixed + beta * beta * old)
     answer = answer + step_size * direction
@@ -464,13 +505,18 @@
     for h in range(halves):
         solution_ref[:, half(h)] = rows_ref[pl.ds(h, NB_DEV, stride=halves), :]
 
-    group_wait(first_in, 1, first_send, near, sends_far, False)
-    for it in range(ITERS):
-        group_wait(field_in[it], held, field_send.at[it], near, takes_far, False)
-        if it < ITERS - 1:
-            group_wait(part_in[it], 1, part_send.at[it], near, sends_far, False)
-    for it in range(ITERS + 1):
-        scal_all(it).wait_send()
+    group_wait(first_in, 1, first_send, by_pair, sends_far, False)
+    for it in range(ITERS - 1):
+        group_wait(part_in[it], 1, part_send.at[it], by_pair, sends_far, False)
+    for it in (ITERS - 1, ITERS):
+        scal_wait(it, n - 1, False)
+
+    @pl.when(sums_here)
+    def _():
+        for it in range(ITERS):
+            group_wait(part_in[0], 1, field_send.at[it], by_sub, takes_far, False)
+        for it in range(ITERS - 1):
+            scal_wait(it, n - 1, False)
 
 
 def per_device(n_slab, n_sub, values, block_ids, tile_counts, right_side):
@@ -480,6 +526,8 @@
     n = n_slab * n_sub
     slots = 3 * n_sub
     window = slots * held
+    span = 2 * held
+    pairs = n_sub // 2
     n_terms = round_up(tiles * coupled * halves, LANES)
     loads = tiles // divisor(tiles, 4, 3, 2)
     f32 = jnp.float32
@@ -502,11 +550,11 @@
             vmem((n_terms, LANES), f32),
             vmem((tiles, rows, LANES), f32),
             vmem((tiles, LANES), f32),
-            vmem((slots, 2, held, LANES), f32),
-            vmem((slots, 2, held, LANES), f32),
-            vmem((ITERS - 1, slots, held, LANES), f32),
-            [vmem((slots, held, LANES), f32)] * (ITERS - 1),
-            vmem((ITERS, held, LANES), f32),
+            vmem((3 * pairs, 2, span, LANES), f32),
+            vmem((slots, 2, span, LANES), f32),
+            vmem((ITERS - 1, 3 * pairs, span, LANES), f32),
+            [vmem((slots, span, LANES), f32)] * (ITERS - 1),
+            vmem((ITERS, span, LANES), f32),
             [vmem((window, LANES), f32)] * ITERS,
             vmem((ITERS + 1, n, LANES), f32),
             pltpu.SMEM((coupled, tiles), jnp.int32),
@@ -523,6 +571,8 @@
             dma((ITERS + 1,)),
             dma((ITERS + 1,)),
             pltpu.SemaphoreType.REGULAR((max(1, n_slab // 2 - 1),)),
+            *([vmem((span, LANES), f32)] * 5),
+            vmem((1, LANES), f32),
         ],
         compiler_params=pltpu.CompilerParams(
             collective_id=0, has_side_effects=True, vmem_limit_bytes=48 * 1024 * 1024

time: 52.5 us -> 49 us (0.933)
  Pallas kernels: 48.4 us -> 44.8 us
    pallas_call x1, Pallas kernels: 48.4 us -> 44.8 us  [per_device(): pl.pallas_call(functools.partial(kernel, n_slab, n_sub), out_shape=(jax.S...]
where the time goes in v3:
time: 49 us; the launch traced here: 48.7 us
  Pallas kernels  44.8 us (91%)
  local copies, waits for them, and re-layouts  2.59 us (5%)
  between operations  1.29 us (3%)
    pallas_call x1, Pallas kernels, per_device(): pl.pallas_call(functools.partial(kernel, n_slab, n_sub), out_shape=(jax.S...  44.8 us
    unnamed x6, local copies, waits for them, and re-layouts  2.59 us

profile of v3, /device:TPU:0, one launch (start us, length us, event | category | flops | bytes accessed | tf_op | source)
XLA Modules:
  0.0 48.7 jit_solution(7891232814636820955)
XLA Ops:
  1.3 0.0 copy-start
  1.3 0.7 %copy-done = f32[24,128]{1,0:T(8,128)S(1)} copy-done((f32[24,128]{1,0:T(8,128)S(1)}, f32[24,128]{1,0:T(8,128)}, u32[]{:S(2)}) %copy-start) | copy-done | bytes 12312
  2.0 0.0 copy-start.1
  2.0 0.7 %copy-done.1 = s32[24,2]{0,1:T(2,128)S(1)} copy-done((s32[24,2]{0,1:T(2,128)S(1)}, s32[24,2]{0,1:T(2,128)}, u32[]{:S(2)}) %copy-start.1) | copy-done | bytes 216
  2.7 44.8 %shard_map.59 = (f32[12,256]{1,0:T(8,128)S(1)}, f32[24,128]{1,0:T(8,128)S(1)}) custom-call(f32[24,2,128,256]{3,2,1,0:T(8,128)} %values_hbm.1, s32[2,24]{1,0:T(2,128)S(1)} %bitcast.1, s32[1,1]{1,0:T(1,128)S(6)} %copy.8.counts_hbm, f32[24,128]{1,0:T(8,128)S(1)} %copy-done), custom_call_target="tpu_custom_call" | custom-call | tf_op jit(solution)/shard_map/pallas_call | solution.py:537
  47.5 0.6 %copy.9 = f32[12,256]{1,0:T(8,128)} copy(f32[12,256]{1,0:T(8,128)S(1)} %get-tuple-element.4) | data formatting | bytes 24576
  48.1 0.6 %copy.10 = f32[24,128]{1,0:T(8,128)} copy(f32[24,128]{1,0:T(8,128)S(1)} %get-tuple-element.5) | data formatting | bytes 24576
Async XLA Ops:
  1.3 0.7 %copy-start = (f32[24,128]{1,0:T(8,128)S(1)}, f32[24,128]{1,0:T(8,128)}, u32[]{:S(2)}) copy-start(f32[24,128]{1,0:T(8,128)} %right_hbm.1) | copy-start | bytes 36868
  2.0 0.7 %copy-start.1 = (s32[24,2]{0,1:T(2,128)S(1)}, s32[24,2]{0,1:T(2,128)}, u32[]{:S(2)}) copy-start(s32[24,2]{0,1:T(2,128)} %param.5) | copy-start | bytes 580

commit v4 on v3

--- a/solution.py
+++ b/solution.py
@@ -12,6 +12,10 @@
 LANES = 128
 SUMS = 3
 STEP = 12
+ORDER = 2
+AHEAD = 4
+GROUP = 4
+SUBLANES = 8
 MESH = pl.DeviceIdType.MESH
 
 
@@ -107,7 +111,8 @@
         part = pl.ds(g * group, group)
         return pltpu.make_async_copy(values_hbm.at[part], values.at[part], load_sem.at[g])
 
-    for g in range(loads):
+    ahead = min(AHEAD, loads)
+    for g in range(ahead):
         load(g).start()
 
     def other(j):
@@ -186,18 +191,26 @@
     def half(h):
         return slice(h * LANES, (h + 1) * LANES)
 
+    bands = rows // SUBLANES
+
+    def band(r):
+        return pl.ds(r * SUBLANES, SUBLANES)
+
     def term_row(k, h, t):
         return pl.ds((k * halves + h) * tiles + t, 1)
 
-    @pl.loop(0, tiles // group)
-    def _(g):
+    def spread_right(g):
         for i in range(group):
             t = g * group + i
-            alive = right_ref[pl.ds(t, 1), :] * live(t)
-            residual_ref[pl.ds(t, 1), :] = alive
-            cols[t] = jnp.broadcast_to(
-                jnp.sum(eye * alive, axis=1, keepdims=True), (rows, LANES)
-            )
+            row = right_ref[pl.ds(t, 1), :] * live(t)
+            residual_ref[pl.ds(t, 1), :] = row
+            for r in range(bands):
+                cols[t, band(r), :] = jnp.broadcast_to(
+                    jnp.sum(eye[r * SUBLANES : (r + 1) * SUBLANES] * row, axis=1, keepdims=True),
+                    (SUBLANES, LANES),
+                )
+
+    spread_right(0)
 
     def scatter(ref):
         full = ref[...]
@@ -330,17 +343,28 @@
     @pl.loop(0, loads)
     def _(g):
         load(g).wait()
+        pl.when(g + ahead < loads)(lambda: load(g + ahead).start())
         for i in range(group):
             t = g * group + i
             alive = live(t)
-            right = cols[t]
+            n_sums = coupled * halves
+            sums = [None] * (2 * n_sums)
+            for r in range(bands):
+                right = cols[t, band(r), :]
+                for k in range(coupled):
+                    for h in range(halves):
+                        j = k * halves + h
+                        a = values[t, k, band(r), half(h)]
+                        sums[j] = a * right if r == 0 else sums[j] + a * right
+                        sums[n_sums + j] = a * a if r == 0 else sums[n_sums + j] + a * a
             for k in range(coupled):
                 for h in range(halves):
-                    a = values[t, k, :, half(h)]
-                    terms[term_row(k, h, t), :] = jnp.sum(a * right, axis=0, keepdims=True)
+                    j = k * halves + h
+                    terms[term_row(k, h, t), :] = jnp.sum(sums[j], axis=0, keepdims=True)
                     squares[term_row(k, h, t), :] = (
-                        jnp.sum(a * a, axis=0, keepdims=True) * alive
+                        jnp.sum(sums[n_sums + j], axis=0, keepdims=True) * alive
                     )
+        spread_right(jnp.minimum(g + 1, loads - 1))
 
     for i, ref in enumerate((terms, squares)):
         first_out[:, i] = scatter(ref)
@@ -373,25 +397,42 @@
         fields = field_in[it]
         group_wait(fields, span, field_recv.at[it], by_pair, sends_far, True)
 
-        def reduced(t):
+        def picked(t):
             alive = live(t)
+            return [
+                jnp.broadcast_to(
+                    fields[pl.ds(wid[t, k] + h, 1), :] * alive, (SUBLANES, LANES)
+                )
+                for k in range(coupled)
+                for h in range(halves)
+            ]
+
+        def reduced(t, r, row):
             m = None
             for k in range(coupled):
                 for h in range(halves):
-                    picked = fields[pl.ds(wid[t, k] + h, 1), :] * alive
-                    product = values[t, k, :, half(h)] * picked
+                    product = values[t, k, band(r), half(h)] * row[k * halves + h]
                     m = product if m is None else m + product
-            return jnp.broadcast_to(jnp.sum(m, axis=1, keepdims=True), (rows, LANES))
+            return jnp.broadcast_to(jnp.sum(m, axis=1, keepdims=True), (SUBLANES, LANES))
 
         def forward(t):
-            cols[t] = reduced(t)
+            row = picked(t)
+            for r in range(bands):
+                cols[t, band(r), :] = reduced(t, r, row)
 
         def backward(t):
-            image = cols[t]
+            sums = [None] * (coupled * halves)
+            for r in range(bands):
+                image = cols[t, band(r), :]
+                for k in range(coupled):
+                    for h in range(halves):
+                        i = k * halves + h
+                        product = values[t, k, band(r), half(h)] * image
+                        sums[i] = product if r == 0 else sums[i] + product
             for k in range(coupled):
                 for h in range(halves):
                     terms[term_row(k, h, t), :] = jnp.sum(
-                        values[t, k, :, half(h)] * image, axis=0, keepdims=True
+                        sums[k * halves + h], axis=0, keepdims=True
                     )
 
         step = divisor(tiles, STEP, 3, 2)
@@ -400,25 +441,56 @@
             def turned_step(g, turned):
                 for i in range(step):
                     t = g * step + i
-                    turned = jnp.where(lane_row == t, reduced(t), turned)
+                    row = picked(t)
+                    here = lane_row == t
+                    turned = [
+                        jnp.where(here, reduced(t, r, row), turned[r]) for r in range(bands)
+                    ]
                 return turned
 
             image_t = turn(image)
             turned = turn(scaled_image)
-            pushed = lax.fori_loop(0, tiles // step, turned_step, jnp.zeros((rows, LANES), f32))
+            pushed = jnp.concatenate(
+                lax.fori_loop(
+                    0,
+                    tiles // step,
+                    turned_step,
+                    [jnp.zeros((SUBLANES, LANES), f32)] * bands,
+                ),
+                axis=0,
+            )
         else:
-            for i in range(step):
-                forward(i)
-
-            @pl.loop(1, tiles // step)
-            def _(g):
+            if ORDER == 2:
+
+                @pl.loop(0, tiles // step)
+                def _(g):
+                    for i in range(step):
+                        forward(g * step + i)
+
+                @pl.loop(0, tiles // step)
+                def _(g):
+                    for i in range(step):
+                        backward(g * step + i)
+
+            else:
                 for i in range(step):
-                    backward((g - 1) * step + i)
+                    forward(i)
+
+                @pl.loop(1, tiles // step)
+                def _(g):
+                    for i in range(step):
+                        if ORDER == 0:
+                            backward((g - 1) * step + i)
+                        else:
+                            forward(g * step + i)
+                    for i in range(step):
+                        if ORDER == 1:
+                            backward((g - 1) * step + i)
+                        else:
+                            forward(g * step + i)
+
                 for i in range(step):
-                    forward(g * step + i)
-
-            for i in range(step):
-                backward(tiles - step + i)
+                    backward(tiles - step + i)
             part_out[it] = scatter(terms)
             part_start(part_out.at[it], part_in[it], part_send.at[it], part_recv.at[it])
 
@@ -529,7 +601,7 @@
     span = 2 * held
     pairs = n_sub // 2
     n_terms = round_up(tiles * coupled * halves, LANES)
-    loads = tiles // divisor(tiles, 4, 3, 2)
+    loads = tiles // divisor(tiles, GROUP, 3, 2)
     f32 = jnp.float32
     vmem = pltpu.VMEM
     dma = pltpu.SemaphoreType.DMA
@@ -577,7 +649,7 @@
         compiler_params=pltpu.CompilerParams(
             collective_id=0, has_side_effects=True, vmem_limit_bytes=48 * 1024 * 1024
         ),
-    )(values, block_ids.T, tile_counts, right_side)
+    )(values, pltpu.with_memory_space_constraint(block_ids.T, pltpu.HBM), tile_counts, pltpu.with_memory_space_constraint(right_side, pltpu.HBM))
 
 
 def solution(mesh):

time: 49 us -> 48.3 us (0.986)
  local copies, waits for them, and re-layouts: 2.59 us -> 1.21 us
  Pallas kernels: 44.8 us -> 45.7 us
    unnamed x6 -> x2, local copies, waits for them, and re-layouts: 2.59 us -> 1.21 us
    pallas_call x1, Pallas kernels: 44.8 us -> 45.7 us  [per_device(): pl.pallas_call(functools.partial(kernel, n_slab, n_sub), out_shape=(jax.S...]
where the time goes in v4:
time: 48.3 us; the launch traced here: 48.1 us
  Pallas kernels  45.7 us (95%)
  between operations  1.28 us (3%)
  local copies, waits for them, and re-layouts  1.21 us (3%)
    pallas_call x1, Pallas kernels, per_device(): pl.pallas_call(functools.partial(kernel, n_slab, n_sub), out_shape=(jax.S...  45.7 us
    unnamed x2, local copies, waits for them, and re-layouts  1.21 us

profile of v4, /device:TPU:0, one launch (start us, length us, event | category | flops | bytes accessed | tf_op | source)
XLA Modules:
  0.0 48.1 jit_solution(6735814864962476441)
XLA Ops:
  1.3 45.7 %shard_map.59 = (f32[12,256]{1,0:T(8,128)S(1)}, f32[24,128]{1,0:T(8,128)S(1)}) custom-call(f32[24,2,128,256]{3,2,1,0:T(8,128)} %values_hbm.1, s32[2,24]{1,0:T(2,128)} %bitcast.1, s32[1,1]{1,0:T(1,128)S(6)} %copy.8.counts_hbm, f32[24,128]{1,0:T(8,128)} %right_hbm.1), custom_call_target="tpu_custom_call" | custom-call | tf_op jit(solution)/shard_map/pallas_call | solution.py:609
  46.9 0.6 %copy.9 = f32[12,256]{1,0:T(8,128)} copy(f32[12,256]{1,0:T(8,128)S(1)} %get-tuple-element.4) | data formatting | bytes 24576
  47.5 0.6 %copy.10 = f32[24,128]{1,0:T(8,128)} copy(f32[24,128]{1,0:T(8,128)S(1)} %get-tuple-element.5) | data formatting | bytes 24576

commit v5 on v4

--- a/solution.py
+++ b/solution.py
@@ -13,6 +13,7 @@
 SUMS = 3
 STEP = 12
 ORDER = 2
+LAST = 24
 AHEAD = 4
 GROUP = 4
 SUBLANES = 8
@@ -237,16 +238,13 @@
                 (to_slab, 2 * target + 1),
             ).start()
 
-        @pl.when(sends_far)
-        def _():
-            for step in range(1, pairs + 1):
-                one(2, far_rel, far_out, step)
-
         for step in range(1, pairs + 1):
+            pl.when(sends_far)(lambda: one(2, far_rel, far_out, step))
             one(0, 1, kept, step)
-        for step in range(1, pairs):
-            one(1, own_rel, slab, step)
-        pl.when(rests_here)(lambda: one(1, own_rel, slab, pairs))
+            if step < pairs:
+                one(1, own_rel, slab, step)
+            else:
+                pl.when(rests_here)(lambda: one(1, own_rel, slab, pairs))
 
         @pl.when(sums_here)
         def _():
@@ -260,18 +258,19 @@
                 src, in_ref.at[pl.ds(at, span)], send.at[sem], recv.at[sem], (to_slab, target)
             ).start()
 
-        order = [(step, core) for core in range(2) for step in range(1, pairs + 1)]
-
-        @pl.when(takes_far)
-        def _():
-            for step, core in order:
-                one(1, kept - far_in + 1, far_in, step, core)
-
-        for step, core in order:
-            one(0, 1, kept, step, core)
-        for step, core in order:
-            if (step, core) != (pairs, 1):
-                one(0, own_rel, slab, step, core)
+        for core in range(2):
+            steps = range(1, pairs + 1)
+
+            @pl.when(takes_far)
+            def _():
+                for step in steps:
+                    one(1, kept - far_in + 1, far_in, step, core)
+
+            for step in steps:
+                one(0, 1, kept, step, core)
+            for step in steps:
+                if (step, core) != (pairs, 1):
+                    one(0, own_rel, slab, step, core)
 
     def group_wait(ref, per, sem, counts, far_too, recv):
         def wait(i, count):
@@ -340,8 +339,7 @@
         rest = jnp.zeros((LANES - tiles, LANES), f32)
         return jnp.concatenate([x, rest], axis=0).T
 
-    @pl.loop(0, loads)
-    def _(g):
+    def gather(g):
         load(g).wait()
         pl.when(g + ahead < loads)(lambda: load(g + ahead).start())
         for i in range(group):
@@ -364,7 +362,13 @@
                     squares[term_row(k, h, t), :] = (
                         jnp.sum(sums[n_sums + j], axis=0, keepdims=True) * alive
                     )
-        spread_right(jnp.minimum(g + 1, loads - 1))
+
+    @pl.loop(0, loads - 1)
+    def _(g):
+        gather(g)
+        spread_right(g + 1)
+
+    gather(loads - 1)
 
     for i, ref in enumerate((terms, squares)):
         first_out[:, i] = scatter(ref)
@@ -438,9 +442,11 @@
         step = divisor(tiles, STEP, 3, 2)
         if last:
 
+            each = divisor(tiles, LAST, 3, 2)
+
             def turned_step(g, turned):
-                for i in range(step):
-                    t = g * step + i
+                for i in range(each):
+                    t = g * each + i
                     row = picked(t)
                     here = lane_row == t
                     turned = [
@@ -453,7 +459,7 @@
             pushed = jnp.concatenate(
                 lax.fori_loop(
                     0,
-                    tiles // step,
+                    tiles // each,
                     turned_step,
                     [jnp.zeros((SUBLANES, LANES), f32)] * bands,
                 ),
@@ -568,6 +574,18 @@
                     row = pack((kept_dir[...] * back[...], scaled[...] * back[...], square))
                 scal_start(it, row + rho_row[...] if it == 0 else row)
 
+    group_wait(first_in, 1, first_send, by_pair, sends_far, False)
+    for it in range(ITERS - 1):
+        group_wait(part_in[it], 1, part_send.at[it], by_pair, sends_far, False)
+    scal_wait(ITERS, n - 1, False)
+
+    @pl.when(sums_here)
+    def _():
+        for it in range(ITERS):
+            group_wait(part_in[0], 1, field_send.at[it], by_sub, takes_far, False)
+        for it in range(ITERS - 1):
+            scal_wait(it, n - 1, False)
+
     scal_take(ITERS - 1)
     new, mixed, old = unpack(ITERS - 1, SUMS)
     step_size = rho / (new + 2.0 * beta * mixed + beta * beta * old)
@@ -577,18 +595,7 @@
     for h in range(halves):
         solution_ref[:, half(h)] = rows_ref[pl.ds(h, NB_DEV, stride=halves), :]
 
-    group_wait(first_in, 1, first_send, by_pair, sends_far, False)
-    for it in range(ITERS - 1):
-        group_wait(part_in[it], 1, part_send.at[it], by_pair, sends_far, False)
-    for it in (ITERS - 1, ITERS):
-        scal_wait(it, n - 1, False)
-
-    @pl.when(sums_here)
-    def _():
-        for it in range(ITERS):
-            group_wait(part_in[0], 1, field_send.at[it], by_sub, takes_far, False)
-        for it in range(ITERS - 1):
-            scal_wait(it, n - 1, False)
+    scal_wait(ITERS - 1, n - 1, False)
 
 
 def per_device(n_slab, n_sub, values, block_ids, tile_counts, right_side):

time: 48.3 us -> 47.9 us (level)
  no operation moved by 1% of the time
where the time goes in v5:
time: 47.9 us; the launch traced here: 47.8 us
  Pallas kernels  45.3 us (95%)
  between operations  1.28 us (3%)
  local copies, waits for them, and re-layouts  1.21 us (3%)
    pallas_call x1, Pallas kernels, per_device(): pl.pallas_call(functools.partial(kernel, n_slab, n_sub), out_shape=(jax.S...  45.3 us
    unnamed x2, local copies, waits for them, and re-layouts  1.21 us

profile of v5, /device:TPU:0, one launch (start us, length us, event | category | flops | bytes accessed | tf_op | source)
XLA Modules:
  0.0 47.8 jit_solution(17018708234574606029)
XLA Ops:
  1.3 45.3 %shard_map.59 = (f32[12,256]{1,0:T(8,128)S(1)}, f32[24,128]{1,0:T(8,128)S(1)}) custom-call(f32[24,2,128,256]{3,2,1,0:T(8,128)} %values_hbm.1, s32[2,24]{1,0:T(2,128)} %bitcast.1, s32[1,1]{1,0:T(1,128)S(6)} %copy.8.counts_hbm, f32[24,128]{1,0:T(8,128)} %right_hbm.1), custom_call_target="tpu_custom_call" | custom-call | tf_op jit(solution)/shard_map/pallas_call | solution.py:616
  46.6 0.6 %copy.9 = f32[12,256]{1,0:T(8,128)} copy(f32[12,256]{1,0:T(8,128)S(1)} %get-tuple-element.4) | data formatting | bytes 24576
  47.2 0.6 %copy.10 = f32[24,128]{1,0:T(8,128)} copy(f32[24,128]{1,0:T(8,128)S(1)} %get-tuple-element.5) | data formatting | bytes 24576

commit v6 on v5

--- a/solution.py
+++ b/solution.py
@@ -154,7 +154,7 @@
 
     @pl.when(jnp.logical_not(takes_far))
     def _():
-        for ref in (first_in, *part_in):
+        for ref in (*first_in, *part_in):
             ref[2 * n_sub :] = jnp.zeros((n_sub,) + ref.shape[1:], f32)
 
     @pl.when(jnp.logical_not(sends_far))
@@ -370,10 +370,10 @@
 
     gather(loads - 1)
 
+    pl.semaphore_wait(barrier, 2 * n_sub - 1 + n_sub * fars)
     for i, ref in enumerate((terms, squares)):
-        first_out[:, i] = scatter(ref)
-    pl.semaphore_wait(barrier, 2 * n_sub - 1 + n_sub * fars)
-    part_start(first_out, first_in, first_send, first_recv)
+        first_out[i][...] = scatter(ref)
+        part_start(first_out[i], first_in[i], first_send.at[i], first_recv.at[i])
     pass_on(0)
     pass_on(1)
     def own_rows(ref):
@@ -387,8 +387,9 @@
 
     @pl.when(sums_here)
     def _():
-        group_wait(first_in, 1, first_recv, by_sub, takes_far, True)
-        sums = jnp.sum(first_in[...], axis=0)
+        for i in range(2):
+            group_wait(first_in[i], 1, first_recv.at[i], by_sub, takes_far, True)
+        sums = [jnp.sum(ref[...], axis=0) for ref in first_in]
         jacobi[...] = 1.0 / (1.0 + sums[1])
         scaled[...] = jacobi[...] * sums[0]
         kept_dir[...] = scaled[...]
@@ -574,7 +575,8 @@
                     row = pack((kept_dir[...] * back[...], scaled[...] * back[...], square))
                 scal_start(it, row + rho_row[...] if it == 0 else row)
 
-    group_wait(first_in, 1, first_send, by_pair, sends_far, False)
+    for i in range(2):
+        group_wait(first_in[i], 1, first_send.at[i], by_pair, sends_far, False)
     for it in range(ITERS - 1):
         group_wait(part_in[it], 1, part_send.at[it], by_pair, sends_far, False)
     scal_wait(ITERS, n - 1, False)
@@ -629,8 +631,8 @@
             vmem((n_terms, LANES), f32),
             vmem((tiles, rows, LANES), f32),
             vmem((tiles, LANES), f32),
-            vmem((3 * pairs, 2, span, LANES), f32),
-            vmem((slots, 2, span, LANES), f32),
+            [vmem((3 * pairs, span, LANES), f32)] * 2,
+            [vmem((slots, span, LANES), f32)] * 2,
             vmem((ITERS - 1, 3 * pairs, span, LANES), f32),
             [vmem((slots, span, LANES), f32)] * (ITERS - 1),
             vmem((ITERS, span, LANES), f32),
@@ -641,8 +643,8 @@
             vmem((tiles, rows), f32),
             dma((3,)),
             dma((loads,)),
-            dma((2,)),
-            dma((2,)),
+            dma((2, 2)),
+            dma((2, 2)),
             dma((ITERS - 1, 2)),
             dma((ITERS - 1, 2)),
             dma((ITERS, 2)),

time: 47.9 us -> 47.9 us (level)
  no operation moved by 1% of the time
where the time goes in v6:
time: 47.9 us; the launch traced here: 47.7 us
  Pallas kernels  45.2 us (94%)
  between operations  1.28 us (3%)
  local copies, waits for them, and re-layouts  1.21 us (3%)
    pallas_call x1, Pallas kernels, per_device(): pl.pallas_call(functools.partial(kernel, n_slab, n_sub), out_shape=(jax.S...  45.2 us
    unnamed x2, local copies, waits for them, and re-layouts  1.21 us

profile of v6, /device:TPU:0, one launch (start us, length us, event | category | flops | bytes accessed | tf_op | source)
XLA Modules:
  0.0 47.7 jit_solution(16613112056966280212)
XLA Ops:
  1.3 45.2 %shard_map.59 = (f32[12,256]{1,0:T(8,128)S(1)}, f32[24,128]{1,0:T(8,128)S(1)}) custom-call(f32[24,2,128,256]{3,2,1,0:T(8,128)} %values_hbm.1, s32[2,24]{1,0:T(2,128)} %bitcast.1, s32[1,1]{1,0:T(1,128)S(6)} %copy.8.counts_hbm, f32[24,128]{1,0:T(8,128)} %right_hbm.1), custom_call_target="tpu_custom_call" | custom-call | tf_op jit(solution)/shard_map/pallas_call | solution.py:618
  46.5 0.6 %copy.9 = f32[12,256]{1,0:T(8,128)} copy(f32[12,256]{1,0:T(8,128)S(1)} %get-tuple-element.4) | data formatting | bytes 24576
  47.1 0.6 %copy.10 = f32[24,128]{1,0:T(8,128)} copy(f32[24,128]{1,0:T(8,128)S(1)} %get-tuple-element.5) | data formatting | bytes 24576
